TPU v7x, 32 devices: a whole 2x2x4 slice. The times are simulated.
32 devices in a mesh: ens: 4 (over z), replica: 2 (over x), model: 4 (over y, core).
Axes of the slice: x: 2, y: 2, z: 4, core: 2. Of those that a mesh axis runs over, the one named last changes fastest.
Arguments:
- slope_up: float32 [8, 768, 3072], P(('ens', 'replica'), None, 'model'), parts along dimension 0, may hold values from -0.875 to 0.875
- slope_down: float32 [8, 3072, 768], P(('ens', 'replica'), 'model'), parts along dimension 0, may hold values from -0.875 to 0.875
- slope_norm: float32 [8, 768], P(('ens', 'replica')), parts along dimension 0, may hold values from -8 to 8
- slope_bias: float32 [8, 768], P(('ens', 'replica')), parts along dimension 0, may hold values from -8 to 8
- param_up: float32 [3072, 3072], P(('ens', 'replica'), 'model'), parts along dimension 0, may hold values from -0.3125 to 0.3125
- param_down: float32 [12288, 768], P(('ens', 'model'), 'replica'), parts along dimension 0, may hold values from -0.15625 to 0.15625
- param_norm: float32 [3072], P(('ens', 'replica')), parts along dimension 0, may hold values from 0.25 to 1.75
- param_bias: float32 [3072], P(('ens', 'replica')), parts along dimension 0, may hold values from -3 to 3
Outputs:
- half_up: bfloat16 [3072, 3072], P('ens', 'model'), parts along dimension 0
- half_down: bfloat16 [12288, 768], P(('ens', 'model')), parts along dimension 0
- half_norm: bfloat16 [3072], P('ens'), parts along dimension 0
- half_bias: bfloat16 [3072], P('ens'), parts along dimension 0
- next_up: float32 [3072, 3072], P(('ens', 'replica'), 'model'), parts along dimension 0
- next_down: float32 [12288, 768], P(('ens', 'model'), 'replica'), parts along dimension 0
- next_norm: float32 [3072], P(('ens', 'replica')), parts along dimension 0
- next_bias: float32 [3072], P(('ens', 'replica')), parts along dimension 0
There are 4 independent parts, one for each index of `ens`. A program takes and returns all parts, laid end to end along the dimension named above; each array names one. Nothing has to cross between parts.
All inputs are finite; a program needn't handle non-finite values.
Results may differ from a plain program's by a relative error of at most 0.0004.
Values may be sent and summed in bfloat16 or wider, within the bound.
A program may use at most 64 MiB of HBM per device.

v0:
```python
import functools
import math

import jax
import jax.numpy as jnp
from jax import lax
from jax.experimental import pallas as pl
from jax.experimental.pallas import tpu as pltpu
from jax.sharding import PartitionSpec as P

learn_rate = 0.4
LANES = 128
SPAN = 251.0
MESH = pl.DeviceIdType.MESH


def plain(
    slope_up, slope_down, slope_norm, slope_bias, param_up, param_down, param_norm, param_bias
):
    mean_up, mean_down = (
        lax.psum_scatter(slope_up[0], "replica", scatter_dimension=0, tiled=True),
        lax.psum_scatter(slope_down[0], "replica", scatter_dimension=1, tiled=True),
    )
    whole_norm, whole_bias = lax.psum((slope_norm[0], slope_bias[0]), "replica")
    place = lax.axis_index("replica")
    mean_norm = lax.dynamic_slice_in_dim(
        whole_norm, place * param_norm.shape[0], param_norm.shape[0]
    )
    mean_bias = lax.dynamic_slice_in_dim(
        whole_bias, place * param_bias.shape[0], param_bias.shape[0]
    )
    mean_rate = lax.axis_size("replica") ** (-0.5)
    mean_up = mean_up * mean_rate
    mean_down = mean_down * mean_rate
    mean_norm = mean_norm * mean_rate
    mean_bias = mean_bias * mean_rate
    own_up, own_down, slope_up_norm, slope_down_norm = lax.psum(
        (
            jnp.sum(param_up * param_up, axis=1, keepdims=True),
            jnp.sum(param_down * param_down, axis=0, keepdims=True),
            jnp.sum(mean_up * mean_up, axis=1, keepdims=True),
            jnp.sum(mean_down * mean_down, axis=0, keepdims=True),
        ),
        "model",
    )
    mean_up = mean_up * (jnp.sqrt(own_up) * lax.rsqrt(slope_up_norm + 1e-06))
    mean_down = mean_down * (jnp.sqrt(own_down) * lax.rsqrt(slope_down_norm + 1e-06))
    next_up = param_up - learn_rate * mean_up
    next_down = param_down - learn_rate * mean_down
    next_norm = param_norm - learn_rate * mean_norm
    next_bias = param_bias - learn_rate * mean_bias
    half_up, half_down, half_norm, half_bias = (
        lax.all_gather(next_up.astype(jnp.bfloat16), "replica", axis=0, tiled=True),
        lax.all_gather(next_down.astype(jnp.bfloat16), "replica", axis=1, tiled=True),
        lax.all_gather(next_norm.astype(jnp.bfloat16), "replica", axis=0, tiled=True),
        lax.all_gather(next_bias.astype(jnp.bfloat16), "replica", axis=0, tiled=True),
    )
    return (half_up, half_down, half_norm, half_bias, next_up, next_down, next_norm, next_bias)


def encode(x, factor):
    size = jnp.exp2(SPAN * jnp.sqrt(jnp.abs(x) * factor) - 125.0)
    return jnp.where(x < 0, -size, size).astype(jnp.bfloat16)


def decode(y, most):
    y = y.astype(jnp.float32)
    u = jnp.log(jnp.abs(y)) * (math.log2(math.e) / SPAN) + 125.0 / SPAN
    size = u * u * most
    return jnp.where(y < 0, -size, size)


def kernel(
    models,
    s_up, s_down, s_norm, s_bias, p_up, p_down, p_norm, p_bias,
    half_up, half_down, new_up, new_down, v_norm, v_bias, w_norm, w_bias,
    far, near, param, code, got, scale, got_scale, stat, got_stat,
    far_sem, near_sem, param_sem,
    code_send, code_recv, scale_send, scale_recv, stat_send, stat_recv,
    half_send, half_recv, vec_send, vec_recv,
):
    me, model = lax.axis_index("replica"), lax.axis_index("model")
    other = 1 - me
    share = p_up.shape[0]
    blocks = p_up.shape[1] // LANES
    per = share // LANES
    chunks = 2 * per
    rate = lax.axis_size("replica") ** (-0.5)

    def at(start):
        return pl.ds(pl.multiple_of(start, LANES), LANES)

    def is_up(c):
        return c >= per

    def slope_at(c, who):
        if is_up(c):
            return s_up.at[0, at(who * share + (c - per) * LANES), :]
        return s_down.at[0, :, at(who * share + c * LANES)]

    def own_at(c, up, down):
        if is_up(c):
            return up.at[pl.ds((c - per) * LANES, LANES), :]
        return down.at[:, pl.ds(c * LANES, LANES)]

    def buf(bufs, c):
        return bufs[0].at[c - per] if is_up(c) else bufs[1].at[c]

    def block(bufs, c, k):
        if is_up(c):
            return bufs[0].at[c - per, :, pl.ds(k * LANES, LANES)]
        return bufs[1].at[c, pl.ds(k * LANES, LANES), :]

    def to_row(c, x, fold):
        return fold(x.T if is_up(c) else x, axis=0, keepdims=True)

    def to_block(c, row):
        x = jnp.broadcast_to(row, (LANES, LANES))
        return x.T if is_up(c) else x

    far_load = [pltpu.make_async_copy(slope_at(c, other), buf(far, c), far_sem.at[c]) for c in range(chunks)]
    near_load = [pltpu.make_async_copy(slope_at(c, me), buf(near, c), near_sem.at[c]) for c in range(chunks)]
    param_load = [
        pltpu.make_async_copy(own_at(c, p_up, p_down), buf(param, c), param_sem.at[c])
        for c in range(chunks)
    ]
    new = (new_up, new_down)
    half = (half_up.at[me], half_down.at[me])

    def remote(src, dst, send, recv, where):
        return pltpu.make_async_remote_copy(
            src_ref=src, dst_ref=dst, send_sem=send, recv_sem=recv,
            device_id=where, device_id_type=MESH,
        )

    partner = {"replica": other}
    peers = [{"model": lax.rem(model + d, models)} for d in range(1, models)]
    barrier = pltpu.get_barrier_semaphore()
    for where in [partner] + peers:
        pl.semaphore_signal(barrier, inc=1, device_id=where, device_id_type=MESH)
    for copy in far_load[:2]:
        copy.start()

    code_copy = [remote(buf(code, c), buf(got, c), code_send.at[c], code_recv.at[c], partner) for c in range(chunks)]
    scale_copy = [remote(scale.at[c], got_scale.at[c], scale_send.at[c], scale_recv.at[c], partner) for c in range(chunks)]
    stat_copy = [
        [
            remote(stat.at[c], got_stat.at[c, d], stat_send.at[c, d], stat_recv.at[c, d], where)
            for d, where in enumerate(peers)
        ]
        for c in range(chunks)
    ]
    half_copy = [remote(buf(half, c), buf(half, c), half_send.at[c], half_recv.at[c], partner) for c in range(chunks)]
    vec_copy = [
        remote(src, dst, vec_send.at[i], vec_recv.at[i], partner)
        for i, (src, dst) in enumerate([(s_norm, v_norm), (s_bias, v_bias), (p_norm, w_norm), (p_bias, w_bias)])
    ]

    for c in range(chunks):
        far_load[c].wait()
        if c + 2 < chunks:
            far_load[c + 2].start()
        top = jnp.zeros((LANES, LANES), jnp.float32)
        for k in range(blocks):
            top = jnp.maximum(top, jnp.abs(block(far, c, k)[...]))
        most = jnp.maximum(to_row(c, top, jnp.max), 1e-30)
        scale[c] = jnp.broadcast_to(most, scale.shape[1:])
        factor = to_block(c, 1.0 / most)
        for k in range(blocks):
            block(code, c, k)[...] = encode(block(far, c, k)[...], factor)
        if c == 0:
            pl.semaphore_wait(barrier, models)
        scale_copy[c].start()
        code_copy[c].start()
        if c == 0:
            for copy in vec_copy:
                copy.start()
        near_load[c].start()
        param_load[c].start()

    def reduce(c):
        near_load[c].wait()
        param_load[c].wait()
        scale_copy[c].wait_recv()
        code_copy[c].wait_recv()
        factor = to_block(c, got_scale[c, 0:1, :])
        own = jnp.zeros((LANES, LANES), jnp.float32)
        slope = jnp.zeros((LANES, LANES), jnp.float32)
        for k in range(blocks):
            mean = (block(near, c, k)[...] + decode(block(got, c, k)[...], factor)) * rate
            block(near, c, k)[...] = mean
            slope = slope + mean * mean
            p = block(param, c, k)[...]
            own = own + p * p
        stat[c, 0:1, :] = to_row(c, own, jnp.sum)
        stat[c, 1:2, :] = to_row(c, slope, jnp.sum)
        for copy in stat_copy[c]:
            copy.start()

    def update(c):
        total = stat[c, 0:2, :]
        for d in range(models - 1):
            stat_copy[c][d].wait_recv()
            total = total + got_stat[c, d, 0:2, :]
        ratio = to_block(c, jnp.sqrt(total[0:1]) * lax.rsqrt(total[1:2] + 1e-06))
        for k in range(blocks):
            fresh = block(param, c, k)[...] - learn_rate * (block(near, c, k)[...] * ratio)
            block(new, c, k)[...] = fresh
            block(half, c, k)[...] = fresh.astype(jnp.bfloat16)
        half_copy[c].start()

    for c in range(chunks):
        reduce(c)
        if c > 0:
            update(c - 1)
    update(chunks - 1)

    for copy in vec_copy:
        copy.wait()
    for c in range(chunks):
        scale_copy[c].wait_send()
        code_copy[c].wait_send()
        for copy in stat_copy[c]:
            copy.wait_send()
        half_copy[c].wait()


def store(
    half_up, half_down, new_up, new_down, v_norm, v_bias, w_norm, w_bias,
    s_norm, s_bias, p_norm, p_bias,
    h_up, h_down, h_norm, h_bias, n_up, n_down, n_norm, n_bias, sem,
):
    me = lax.axis_index("replica")
    replicas, per = half_up.shape[:2]
    share = per * LANES
    rate = replicas ** (-0.5)
    copies = []

    def put(src, dst):
        copy = pltpu.make_async_copy(src, dst, sem.at[len(copies)])
        copy.start()
        copies.append(copy)

    for c in range(per):
        part = pl.ds(c * LANES, LANES)
        put(new_up.at[c], n_up.at[part, :])
        put(new_down.at[c], n_down.at[:, part])
        for who in range(replicas):
            part = pl.ds(who * share + c * LANES, LANES)
            put(half_up.at[who, c], h_up.at[part, :])
            put(half_down.at[who, c], h_down.at[:, part])

    def vector(s, v, p, w, h, n):
        mean = (s[0, :] + v[0, :]) * rate
        mine, theirs = p[...], w[...]
        low = jnp.where(me == 0, mine, theirs) - learn_rate * mean[:share]
        high = jnp.where(me == 0, theirs, mine) - learn_rate * mean[share:]
        h[...] = jnp.concatenate([low, high]).astype(jnp.bfloat16)
        n[...] = jnp.where(me == 0, low, high)

    vector(s_norm, v_norm, p_norm, w_norm, h_norm, n_norm)
    vector(s_bias, v_bias, p_bias, w_bias, h_bias, n_bias)
    for copy in copies:
        copy.wait()


def fused(mesh, s_up, s_down, s_norm, s_bias, p_up, p_down, p_norm, p_bias):
    models, replicas = mesh.shape["model"], mesh.shape["replica"]
    width, inner = s_up.shape[1:]
    share = p_up.shape[0]
    per = share // LANES
    chunks = 2 * per
    f32, bf16 = jnp.float32, jnp.bfloat16
    any_spec = pl.BlockSpec(memory_space=pl.ANY)
    vmem = pl.BlockSpec(memory_space=pltpu.VMEM)
    hbm = pl.BlockSpec(memory_space=pltpu.HBM)
    dma = pltpu.SemaphoreType.DMA

    def pair(dtype):
        return (pltpu.VMEM((per, LANES, inner), dtype), pltpu.VMEM((per, inner, LANES), dtype))

    shape = jax.ShapeDtypeStruct
    held = pl.pallas_call(
        functools.partial(kernel, models),
        out_shape=(
            pltpu.VMEM((replicas, per, LANES, inner), bf16),
            pltpu.VMEM((replicas, per, inner, LANES), bf16),
            *pair(f32),
            pltpu.VMEM((1, width), f32),
            pltpu.VMEM((1, width), f32),
            pltpu.VMEM((share,), f32),
            pltpu.VMEM((share,), f32),
        ),
        in_specs=[hbm] * 8,
        out_specs=[vmem] * 8,
        scratch_shapes=[
            pair(f32), pair(f32), pair(f32), pair(bf16), pair(bf16),
            pltpu.VMEM((chunks, 8, LANES), f32), pltpu.VMEM((chunks, 8, LANES), f32),
            pltpu.VMEM((chunks, 8, LANES), f32), pltpu.VMEM((chunks, models - 1, 8, LANES), f32),
            dma((chunks,)), dma((chunks,)), dma((chunks,)),
            dma((chunks,)), dma((chunks,)), dma((chunks,)), dma((chunks,)),
            dma((chunks, models - 1)), dma((chunks, models - 1)),
            dma((chunks,)), dma((chunks,)), dma((4,)), dma((4,)),
        ],
        compiler_params=pltpu.CompilerParams(
            collective_id=0, has_side_effects=True, vmem_limit_bytes=58 * 2**20
        ),
    )(s_up, s_down, s_norm, s_bias, p_up, p_down, p_norm, p_bias)
    return pl.pallas_call(
        store,
        out_shape=(
            shape((width, inner), bf16),
            shape((inner, width), bf16),
            shape((width,), bf16),
            shape((width,), bf16),
            shape((share, inner), f32),
            shape((inner, share), f32),
            shape((share,), f32),
            shape((share,), f32),
        ),
        in_specs=[vmem] * 12,
        out_specs=[any_spec, any_spec, vmem, vmem, any_spec, any_spec, vmem, vmem],
        scratch_shapes=[dma(((2 + 2 * replicas) * per,))],
        compiler_params=pltpu.CompilerParams(
            has_side_effects=True, vmem_limit_bytes=16 * 2**20
        ),
    )(*held, s_norm, s_bias, p_norm, p_bias)


def solution(mesh):
    in_specs = (
        P(("ens", "replica"), None, "model"),
        P(("ens", "replica"), "model", None),
        P(("ens", "replica"), None),
        P(("ens", "replica"), None),
        P(("ens", "replica"), "model"),
        P(("ens", "model"), "replica"),
        P(("ens", "replica")),
        P(("ens", "replica")),
    )
    out_specs = (
        P("ens", "model"),
        P(("ens", "model"), None),
        P("ens"),
        P("ens"),
        P(("ens", "replica"), "model"),
        P(("ens", "model"), "replica"),
        P(("ens", "replica")),
        P(("ens", "replica")),
    )

    def on_device(*args):
        share, inner = args[4].shape
        if mesh.shape["replica"] == 2 and share % LANES == 0 and inner % LANES == 0:
            return fused(mesh, *args)
        return plain(*args)

    return jax.shard_map(
        on_device, mesh=mesh, in_specs=in_specs, out_specs=out_specs, check_vma=False
    )
```

profile of v0, /device:TPU:1, one launch (start us, length us, event | category | flops | bytes accessed | tf_op | source)
XLA Modules:
  0.0 60.4 jit_solution(587304067080238905)
XLA Ops:
  0.6 0.0 copy-start.3
  0.6 0.0 copy-start.2
  0.7 0.0 copy-start.1
  0.7 0.0 copy-start
  0.7 56.7 %shard_map.143 = (bf16[2,3,128,768]{3,2,1,0:T(8,128)(2,1)S(1)}, bf16[2,3,768,128]{3,2,1,0:T(8,128)(2,1)S(1)}, f32[3,128,768]{2,1,0:T(8,128)S(1)}, f32[3,768,128]...) custom-call(f32[1,768,768]{2,1,0:T(8,128)} %s_up.1, ...), custom_call_target="tpu_custom_call" | custom-call | tf_op jit(solution)/shard_map/pallas_call | solution.py:283
  57.4 0.0 copy-done.3
  57.4 0.0 copy-done.2
  57.4 0.0 copy-done.1
  57.4 0.0 copy-done
  57.5 2.9 %shard_map.144 = (bf16[768,768]{1,0:T(8,128)(2,1)}, bf16[768,768]{1,0:T(8,128)(2,1)}, bf16[768]{0:T(1024)(128)(2,1)}, bf16[768]{0:T(1024)(128)(2,1)}, f32[384,76...) custom-call(bf16[2,3,128,768]{3,2,1,0:T(8,128)(2,1)S(1)} %get-tuple-element.16.half_up, ...), custom_call_target="tpu_custom_call" | custom-call | tf_op jit(solution)/shard_map/pallas_call | solution.py:309
Async XLA Ops:
  0.6 56.8 %copy-start.3 = (f32[384]{0:T(512)S(1)}, f32[384]{0:T(512)}, u32[]{:S(2)}) copy-start(f32[384]{0:T(512)} %p_bias.3) | copy-start | bytes 4612
  0.6 56.8 %copy-start.2 = (f32[384]{0:T(512)S(1)}, f32[384]{0:T(512)}, u32[]{:S(2)}) copy-start(f32[384]{0:T(512)} %p_norm.3) | copy-start | bytes 4612
  0.7 56.8 %copy-start.1 = (f32[1,768]{1,0:T(1,128)S(1)}, f32[1,768]{1,0:T(1,128)}, u32[]{:S(2)}) copy-start(f32[1,768]{1,0:T(1,128)} %s_bias.3) | copy-start | bytes 9220
  0.7 56.8 %copy-start = (f32[1,768]{1,0:T(1,128)S(1)}, f32[1,768]{1,0:T(1,128)}, u32[]{:S(2)}) copy-start(f32[1,768]{1,0:T(1,128)} %s_norm.3) | copy-start | bytes 9220
where the time goes:
time: 61.5 us; the launch traced here: 60.4 us
  Pallas kernels  59.6 us (97%)
  between operations  0.71 us (1%)
    pallas_call x1, Pallas kernels, fused(): pl.pallas_call(functools.partial(kernel, models), out_shape=(pltpu.VMEM((...  56.7 us
    pallas_call x1, Pallas kernels, fused(): pl.pallas_call(store, out_shape=(shape((width, inner), bf16), shape((inne...  2.9 us

commit v1 on v0

--- a/solution.py
+++ b/solution.py
@@ -73,9 +73,9 @@
 def kernel(
     models,
     s_up, s_down, s_norm, s_bias, p_up, p_down, p_norm, p_bias,
-    half_up, half_down, new_up, new_down, v_norm, v_bias, w_norm, w_bias,
-    far, near, param, code, got, scale, got_scale, stat, got_stat,
-    far_sem, near_sem, param_sem,
+    half_up, half_down, new_up, new_down, h_norm, h_bias, n_norm, n_bias,
+    far, near, param, code, got, scale, got_scale, stat, got_stat, mine, theirs,
+    far_sem, near_sem, param_sem, vec_sem,
     code_send, code_recv, scale_send, scale_recv, stat_send, stat_recv,
     half_send, half_recv, vec_send, vec_recv,
 ):
@@ -151,9 +151,11 @@
         for c in range(chunks)
     ]
     half_copy = [remote(buf(half, c), buf(half, c), half_send.at[c], half_recv.at[c], partner) for c in range(chunks)]
+    vectors = (s_norm, s_bias, p_norm, p_bias)
+    vec_load = [pltpu.make_async_copy(src, mine[i], vec_sem.at[i]) for i, src in enumerate(vectors)]
     vec_copy = [
-        remote(src, dst, vec_send.at[i], vec_recv.at[i], partner)
-        for i, (src, dst) in enumerate([(s_norm, v_norm), (s_bias, v_bias), (p_norm, w_norm), (p_bias, w_bias)])
+        remote(src, theirs[i], vec_send.at[i], vec_recv.at[i], partner)
+        for i, src in enumerate(vectors)
     ]
 
     for c in range(chunks):
@@ -164,7 +166,7 @@
         for k in range(blocks):
             top = jnp.maximum(top, jnp.abs(block(far, c, k)[...]))
         most = jnp.maximum(to_row(c, top, jnp.max), 1e-30)
-        scale[c] = jnp.broadcast_to(most, scale.shape[1:])
+        scale[c] = most
         factor = to_block(c, 1.0 / most)
         for k in range(blocks):
             block(code, c, k)[...] = encode(block(far, c, k)[...], factor)
@@ -173,7 +175,7 @@
         scale_copy[c].start()
         code_copy[c].start()
         if c == 0:
-            for copy in vec_copy:
+            for copy in vec_copy + vec_load:
                 copy.start()
         near_load[c].start()
         param_load[c].start()
@@ -183,7 +185,7 @@
         param_load[c].wait()
         scale_copy[c].wait_recv()
         code_copy[c].wait_recv()
-        factor = to_block(c, got_scale[c, 0:1, :])
+        factor = to_block(c, got_scale[c])
         own = jnp.zeros((LANES, LANES), jnp.float32)
         slope = jnp.zeros((LANES, LANES), jnp.float32)
         for k in range(blocks):
@@ -215,8 +217,18 @@
             update(c - 1)
     update(chunks - 1)
 
-    for copy in vec_copy:
-        copy.wait()
+    def vector(i, h, n):
+        for copy in (vec_load[i], vec_load[i + 2], vec_copy[i], vec_copy[i + 2]):
+            copy.wait()
+        mean = (mine[i][0, :] + theirs[i][0, :]) * rate
+        here, there = mine[i + 2][...], theirs[i + 2][...]
+        low = jnp.where(me == 0, here, there) - learn_rate * mean[:share]
+        high = jnp.where(me == 0, there, here) - learn_rate * mean[share:]
+        h[...] = jnp.concatenate([low, high]).astype(jnp.bfloat16)
+        n[...] = jnp.where(me == 0, low, high)
+
+    vector(0, h_norm, n_norm)
+    vector(1, h_bias, n_bias)
     for c in range(chunks):
         scale_copy[c].wait_send()
         code_copy[c].wait_send()
@@ -226,14 +238,11 @@
 
 
 def store(
-    half_up, half_down, new_up, new_down, v_norm, v_bias, w_norm, w_bias,
-    s_norm, s_bias, p_norm, p_bias,
+    half_up, half_down, new_up, new_down, k_norm, k_bias, m_norm, m_bias,
     h_up, h_down, h_norm, h_bias, n_up, n_down, n_norm, n_bias, sem,
 ):
-    me = lax.axis_index("replica")
     replicas, per = half_up.shape[:2]
     share = per * LANES
-    rate = replicas ** (-0.5)
     copies = []
 
     def put(src, dst):
@@ -249,17 +258,8 @@
             part = pl.ds(who * share + c * LANES, LANES)
             put(half_up.at[who, c], h_up.at[part, :])
             put(half_down.at[who, c], h_down.at[:, part])
-
-    def vector(s, v, p, w, h, n):
-        mean = (s[0, :] + v[0, :]) * rate
-        mine, theirs = p[...], w[...]
-        low = jnp.where(me == 0, mine, theirs) - learn_rate * mean[:share]
-        high = jnp.where(me == 0, theirs, mine) - learn_rate * mean[share:]
-        h[...] = jnp.concatenate([low, high]).astype(jnp.bfloat16)
-        n[...] = jnp.where(me == 0, low, high)
-
-    vector(s_norm, v_norm, p_norm, w_norm, h_norm, n_norm)
-    vector(s_bias, v_bias, p_bias, w_bias, h_bias, n_bias)
+    for src, dst in ((k_norm, h_norm), (k_bias, h_bias), (m_norm, n_norm), (m_bias, n_bias)):
+        put(src, dst)
     for copy in copies:
         copy.wait()
 
@@ -279,6 +279,10 @@
     def pair(dtype):
         return (pltpu.VMEM((per, LANES, inner), dtype), pltpu.VMEM((per, inner, LANES), dtype))
 
+    vecs = (
+        pltpu.VMEM((1, width), f32), pltpu.VMEM((1, width), f32),
+        pltpu.VMEM((share,), f32), pltpu.VMEM((share,), f32),
+    )
     shape = jax.ShapeDtypeStruct
     held = pl.pallas_call(
         functools.partial(kernel, models),
@@ -286,8 +290,8 @@
             pltpu.VMEM((replicas, per, LANES, inner), bf16),
             pltpu.VMEM((replicas, per, inner, LANES), bf16),
             *pair(f32),
-            pltpu.VMEM((1, width), f32),
-            pltpu.VMEM((1, width), f32),
+            pltpu.VMEM((width,), bf16),
+            pltpu.VMEM((width,), bf16),
             pltpu.VMEM((share,), f32),
             pltpu.VMEM((share,), f32),
         ),
@@ -295,9 +299,10 @@
         out_specs=[vmem] * 8,
         scratch_shapes=[
             pair(f32), pair(f32), pair(f32), pair(bf16), pair(bf16),
-            pltpu.VMEM((chunks, 8, LANES), f32), pltpu.VMEM((chunks, 8, LANES), f32),
+            pltpu.VMEM((chunks, 1, LANES), f32), pltpu.VMEM((chunks, 1, LANES), f32),
             pltpu.VMEM((chunks, 8, LANES), f32), pltpu.VMEM((chunks, models - 1, 8, LANES), f32),
-            dma((chunks,)), dma((chunks,)), dma((chunks,)),
+            vecs, vecs,
+            dma((chunks,)), dma((chunks,)), dma((chunks,)), dma((4,)),
             dma((chunks,)), dma((chunks,)), dma((chunks,)), dma((chunks,)),
             dma((chunks, models - 1)), dma((chunks, models - 1)),
             dma((chunks,)), dma((chunks,)), dma((4,)), dma((4,)),
@@ -318,13 +323,13 @@
             shape((share,), f32),
             shape((share,), f32),
         ),
-        in_specs=[vmem] * 12,
-        out_specs=[any_spec, any_spec, vmem, vmem, any_spec, any_spec, vmem, vmem],
-        scratch_shapes=[dma(((2 + 2 * replicas) * per,))],
+        in_specs=[vmem] * 8,
+        out_specs=[any_spec] * 8,
+        scratch_shapes=[dma(((2 + 2 * replicas) * per + 4,))],
         compiler_params=pltpu.CompilerParams(
             has_side_effects=True, vmem_limit_bytes=16 * 2**20
         ),
-    )(*held, s_norm, s_bias, p_norm, p_bias)
+    )(*held)
 
 
 def solution(mesh):

time: 61.5 us -> 60.4 us (0.982)
  Pallas kernels: 59.6 us -> 58.7 us
where the time goes in v1:
time: 60.4 us; the launch traced here: 59.3 us
  Pallas kernels  58.7 us (97%)
  between operations  0.64 us (1%)
    pallas_call x1, Pallas kernels, fused(): pl.pallas_call(functools.partial(kernel, models), out_shape=(pltpu.VMEM((...  56.3 us
    pallas_call x1, Pallas kernels, fused(): pl.pallas_call(store, out_shape=(shape((width, inner), bf16), shape((inne...  2.36 us

profile of v1, /device:TPU:1, one launch (start us, length us, event | category | flops | bytes accessed | tf_op | source)
XLA Modules:
  0.0 59.3 jit_solution(10223477364462091396)
XLA Ops:
  0.6 56.3 %shard_map.143 = (bf16[2,3,128,768]{3,2,1,0:T(8,128)(2,1)S(1)}, bf16[2,3,768,128]{3,2,1,0:T(8,128)(2,1)S(1)}, f32[3,128,768]{2,1,0:T(8,128)S(1)}, f32[3,768,128]...) custom-call(f32[1,768,768]{2,1,0:T(8,128)} %s_up.1, ...), custom_call_target="tpu_custom_call" | custom-call | tf_op jit(solution)/shard_map/pallas_call | solution.py:287
  56.9 2.4 %shard_map.144 = (bf16[768,768]{1,0:T(8,128)(2,1)}, bf16[768,768]{1,0:T(8,128)(2,1)}, bf16[768]{0:T(1024)(128)(2,1)}, bf16[768]{0:T(1024)(128)(2,1)}, f32[384,76...) custom-call(bf16[2,3,128,768]{3,2,1,0:T(8,128)(2,1)S(1)} %get-tuple-element.16.half_up, ...), custom_call_target="tpu_custom_call" | custom-call | tf_op jit(solution)/shard_map/pallas_call | solution.py:314

commit v2 on v1

--- a/solution.py
+++ b/solution.py
@@ -74,7 +74,7 @@
     models,
     s_up, s_down, s_norm, s_bias, p_up, p_down, p_norm, p_bias,
     half_up, half_down, new_up, new_down, h_norm, h_bias, n_norm, n_bias,
-    far, near, param, code, got, scale, got_scale, stat, got_stat, mine, theirs,
+    far, near, param, code, got, scale, got_scale, stat, got_stat, mine, theirs, ready,
     far_sem, near_sem, param_sem, vec_sem,
     code_send, code_recv, scale_send, scale_recv, stat_send, stat_recv,
     half_send, half_recv, vec_send, vec_recv,
@@ -136,10 +136,38 @@
     partner = {"replica": other}
     peers = [{"model": lax.rem(model + d, models)} for d in range(1, models)]
     barrier = pltpu.get_barrier_semaphore()
-    for where in [partner] + peers:
-        pl.semaphore_signal(barrier, inc=1, device_id=where, device_id_type=MESH)
+
+    def signal(sem, where):
+        pl.semaphore_signal(sem, inc=1, device_id=where, device_id_type=MESH)
+
+    @pl.when(me == 0)
+    def _():
+        signal(barrier, partner)
+
     for copy in far_load[:2]:
         copy.start()
+
+    @pl.when(me == 1)
+    def _():
+        pl.semaphore_wait(barrier, 1)
+        signal(ready, partner)
+
+    def meet_partner():
+        @pl.when(me == 0)
+        def _():
+            pl.semaphore_wait(ready, 1)
+            for where in peers:
+                signal(barrier, where)
+
+    def meet_peers():
+        @pl.when(me == 0)
+        def _():
+            pl.semaphore_wait(barrier, models - 1)
+            signal(ready, partner)
+
+        @pl.when(me == 1)
+        def _():
+            pl.semaphore_wait(ready, 1)
 
     code_copy = [remote(buf(code, c), buf(got, c), code_send.at[c], code_recv.at[c], partner) for c in range(chunks)]
     scale_copy = [remote(scale.at[c], got_scale.at[c], scale_send.at[c], scale_recv.at[c], partner) for c in range(chunks)]
@@ -171,7 +199,7 @@
         for k in range(blocks):
             block(code, c, k)[...] = encode(block(far, c, k)[...], factor)
         if c == 0:
-            pl.semaphore_wait(barrier, models)
+            meet_partner()
         scale_copy[c].start()
         code_copy[c].start()
         if c == 0:
@@ -179,6 +207,8 @@
                 copy.start()
         near_load[c].start()
         param_load[c].start()
+
+    meet_peers()
 
     def reduce(c):
         near_load[c].wait()
@@ -301,7 +331,7 @@
             pair(f32), pair(f32), pair(f32), pair(bf16), pair(bf16),
             pltpu.VMEM((chunks, 1, LANES), f32), pltpu.VMEM((chunks, 1, LANES), f32),
             pltpu.VMEM((chunks, 8, LANES), f32), pltpu.VMEM((chunks, models - 1, 8, LANES), f32),
-            vecs, vecs,
+            vecs, vecs, pltpu.SemaphoreType.REGULAR,
             dma((chunks,)), dma((chunks,)), dma((chunks,)), dma((4,)),
             dma((chunks,)), dma((chunks,)), dma((chunks,)), dma((chunks,)),
             dma((chunks, models - 1)), dma((chunks, models - 1)),

time: 60.4 us -> 59.9 us (level)
  the two profiles are of different devices: /device:TPU:1 before, /device:TPU:0 now
where the time goes in v2:
time: 59.9 us; the launch traced here: 59.7 us
  Pallas kernels  59.1 us (99%)
  between operations  0.64 us (1%)
    pallas_call x1, Pallas kernels, fused(): pl.pallas_call(functools.partial(kernel, models), out_shape=(pltpu.VMEM((...  56.7 us
    pallas_call x1, Pallas kernels, fused(): pl.pallas_call(store, out_shape=(shape((width, inner), bf16), shape((inne...  2.36 us

profile of v2, /device:TPU:0, one launch (start us, length us, event | category | flops | bytes accessed | tf_op | source)
XLA Modules:
  0.0 59.7 jit_solution(6223687700149506287)
XLA Ops:
  0.6 56.7 %shard_map.143 = (bf16[2,3,128,768]{3,2,1,0:T(8,128)(2,1)S(1)}, bf16[2,3,768,128]{3,2,1,0:T(8,128)(2,1)S(1)}, f32[3,128,768]{2,1,0:T(8,128)S(1)}, f32[3,768,128]...) custom-call(f32[1,768,768]{2,1,0:T(8,128)} %s_up.1, ...), custom_call_target="tpu_custom_call" | custom-call | tf_op jit(solution)/shard_map/pallas_call | solution.py:317
  57.3 2.4 %shard_map.144 = (bf16[768,768]{1,0:T(8,128)(2,1)}, bf16[768,768]{1,0:T(8,128)(2,1)}, bf16[768]{0:T(1024)(128)(2,1)}, bf16[768]{0:T(1024)(128)(2,1)}, f32[384,76...) custom-call(bf16[2,3,128,768]{3,2,1,0:T(8,128)(2,1)S(1)} %get-tuple-element.16.half_up, ...), custom_call_target="tpu_custom_call" | custom-call | tf_op jit(solution)/shard_map/pallas_call | solution.py:344
